TPU v7x, 32 devices: a whole 2x2x4 slice. The times are simulated.
32 devices in a mesh: lat: 8 (over y, x, core), lev: 4 (over z).
Axes of the slice: x: 2, y: 2, z: 4, core: 2. Of those that a mesh axis runs over, the one named last changes fastest.
Arguments:
- fourier: bfloat16 [64, 2560, 128], P('lev', 'lat'), may hold values from -6 to 6
- quad_weights: float32 [2560], P('lat'), may hold values from 0.005 to 0.05
- legendre: bfloat16 [2560, 64, 1280], P('lat'), may hold values from -6 to 6
- owner_pair: int32 [64], replicated, may hold values from 0 to 63, each once
Outputs:
- spectra: float32 [64, 64, 1280], P('lat', 'lev')
- energy: float32 [], replicated
Inputs may be any that keep to these rules, and one draw needn't show every extreme that they name: `owner_pair`: a permutation of 0 to 63.
All inputs are finite; a program needn't handle non-finite values.
Results may differ from a plain program's by a relative error of at most 0.00094.
Values may be sent and summed in bfloat16 or wider, within the bound.
A program may use at most 192 MiB of HBM per device.

v0:
```python
import functools

import jax
import jax.numpy as jnp
from jax import lax
from jax.experimental import pallas as pl
from jax.experimental.pallas import tpu as pltpu
from jax.sharding import PartitionSpec as P

SPACING = 10
GROUP = 8
HALVES = 2
MESH = pl.DeviceIdType.MESH


def remote(src, dst, send, recv, device):
    return pltpu.make_async_remote_copy(
        src_ref=src, dst_ref=dst, send_sem=send, recv_sem=recv, device_id=device, device_id_type=MESH
    )


def kernel(
    cfg,
    owner_ref,
    wave_ref,
    leg_ref,
    out_ref,
    energy_ref,
    lhs,
    part,
    pair_out,
    pair_in,
    chip_out,
    chip_in,
    esum,
    elat,
    elev,
    pair_send,
    pair_recv,
    chip_send,
    chip_recv,
    elat_send,
    elat_recv,
    elev_send,
    elev_recv,
):
    n_lat, n_lev, ch, lats, pairs, length, width, steps, m_win = cfg
    t = pl.program_id(0)
    h = pl.program_id(1)
    lat = lax.axis_index("lat")
    lev = lax.axis_index("lev")
    core = lax.rem(lat, 2)
    chip = lat // 2
    chips = n_lat // 2
    own = pairs // n_lat
    rows = GROUP * ch
    groups = pairs // GROUP
    half_groups = groups // HALVES
    barrier = pltpu.get_barrier_semaphore()

    @pl.when((t == 0) & (h == 0))
    def _():
        for d in range(1, n_lat):
            pl.semaphore_signal(
                barrier, inc=1, device_id=(lax.rem(lat + d, n_lat), lev), device_id_type=MESH
            )
        for d in range(1, n_lev):
            pl.semaphore_signal(
                barrier, inc=1, device_id=(lat, lax.rem(lev + d, n_lev)), device_id_type=MESH
            )
        esum[...] = jnp.zeros_like(esum)

    @pl.when(t == 0)
    def _():
        def build(step, carry):
            g = h * half_groups + step
            for start in range(0, lats * GROUP, 256):
                size = min(256, lats * GROUP - start)
                first = start // GROUP
                base = first // 128 * 128
                depth = min(128, lats - base)
                src = lax.broadcasted_iota(jnp.int32, (depth, size), 0)
                dst = lax.broadcasted_iota(jnp.int32, (depth, size), 1)
                spread = (src == dst // GROUP + (first - base)).astype(jnp.float32).astype(jnp.bfloat16)
                row = lax.broadcasted_iota(jnp.int32, (rows, size), 0) // ch
                col = lax.rem(lax.broadcasted_iota(jnp.int32, (rows, size), 1), GROUP)
                for side in range(2):
                    j = g * GROUP if side == 0 else m_win - GROUP - g * GROUP
                    w = wave_ref[pl.ds(pl.multiple_of(j * ch, rows), rows), base : base + depth]
                    x = jnp.dot(w, spread, preferred_element_type=jnp.float32)
                    keep = row == (col if side == 0 else GROUP - 1 - col)
                    lhs[g, side * rows : (side + 1) * rows, start : start + size] = jnp.where(
                        keep, x, 0.0
                    ).astype(jnp.bfloat16)
            return carry

        lax.fori_loop(0, half_groups, build, 0)

    slot = lax.rem(t, 2)
    col_ids = t * width + lax.broadcasted_iota(jnp.int32, (ch, width), 1)

    for step in range(half_groups):
        g = h * half_groups + step
        rhs = leg_ref[:, step * GROUP : (step + 1) * GROUP, :].reshape(lats * GROUP, width)
        both = jnp.dot(lhs[g], rhs, preferred_element_type=jnp.float32)
        for i in range(GROUP):
            p = g * GROUP + i
            low = both[i * ch : (i + 1) * ch]
            high = both[rows + (GROUP - 1 - i) * ch : rows + (GROUP - i) * ch]
            limit = length - SPACING * p - SPACING // 2
            part[slot, p] = jnp.where(col_ids < limit, low, high)

    def pair_copy(u):
        return remote(
            pair_out.at[u], pair_in.at[u], pair_send.at[u], pair_recv.at[u],
            (2 * chip + 1 - core, lev),
        )

    def chip_copy(u, d):
        return remote(
            chip_out.at[u, d - 1], chip_in.at[u, d - 1],
            chip_send.at[u, d - 1], chip_recv.at[u, d - 1],
            (2 * lax.rem(chip + d, chips) + core, lev),
        )

    def to_partner(u):
        s = lax.rem(u, 2)
        for d in range(chips):
            q = lax.rem(chip + d, chips)
            for o in range(own):
                pair_id = owner_ref[(2 * q + 1 - core) * own + o]
                pair_out[u, d * own + o] = part[s, pair_id]
        pair_copy(u).start()

    def columns(u):
        return pl.ds(pl.multiple_of(u * width, width), width)

    def to_chips(u):
        s = lax.rem(u, 2)
        pair_copy(u).wait_recv()
        for d in list(range(1, chips)) + [0]:
            q = lax.rem(chip + d, chips)
            for o in range(own):
                pair_id = owner_ref[(2 * q + core) * own + o]
                total = part[s, pair_id] + pair_in[u, d * own + o]
                if d:
                    chip_out[u, d - 1, o] = total.astype(jnp.bfloat16)
                else:
                    out_ref[o, :, columns(u)] = total
            if d:
                chip_copy(u, d).start()

    channel = lev * ch + lax.broadcasted_iota(jnp.int32, (ch, width), 0)
    factor = 1.0 + 2.0 * (channel // 2).astype(jnp.float32) / (ch * n_lev // 2 - 1)

    def collect(u):
        for d in range(1, chips):
            chip_copy(u, d).wait_recv()
        acc = jnp.zeros((ch, width), jnp.float32)
        for o in range(own):
            total = out_ref[o, :, columns(u)]
            for d in range(1, chips):
                total = total + chip_in[u, d - 1, o].astype(jnp.float32)
            out_ref[o, :, columns(u)] = total
            acc = acc + total * total
        esum[...] += acc * factor

    @pl.when((t == 0) & (h == HALVES - 1))
    def _():
        pl.semaphore_wait(barrier, n_lat - 1 + n_lev - 1)

    @pl.when((h == 0) & (t >= 1))
    def _():
        to_chips(t - 1)

    @pl.when(h == HALVES - 1)
    def _():
        to_partner(t)

    @pl.when((h == HALVES - 1) & (t >= 2))
    def _():
        collect(t - 2)

    @pl.when((h == HALVES - 1) & (t == steps - 1))
    def _():
        if steps >= 2:
            collect(steps - 2)
        to_chips(steps - 1)
        collect(steps - 1)

        def exchange(buf, send, recv, me, n, device):
            def copy(idx, d):
                return remote(
                    buf.at[idx], buf.at[idx], send.at[d - 1], recv.at[idx],
                    device(lax.rem(me + d, n)),
                )

            for d in range(1, n):
                copy(me, d).start()
            for d in range(1, n):
                copy(lax.rem(me + n - d, n), d).wait_recv()
            for d in range(1, n):
                copy(me, d).wait_send()

        acc = esum[...]
        lanes = sum(acc[:, i : i + 128] for i in range(0, width, 128))
        elat[lat] = sum(lanes[i : i + 8] for i in range(0, ch, 8))
        exchange(elat, elat_send, elat_recv, lat, n_lat, lambda i: (i, lev))
        total = elat[0]
        for i in range(1, n_lat):
            total = total + elat[i]
        elev[lev] = total
        exchange(elev, elev_send, elev_recv, lev, n_lev, lambda i: (lat, i))
        total = elev[0]
        for i in range(1, n_lev):
            total = total + elev[i]
        energy_ref[...] = jnp.full((1, 1), jnp.sum(total)) / (pairs * ch * n_lev * length)

        for u in range(steps):
            pair_copy(u).wait_send()
            for d in range(1, chips):
                chip_copy(u, d).wait_send()


def shards(n_lat, n_lev, fourier, quad_weights, legendre, owner_pair):
    weighted = (fourier.astype(jnp.float32) * quad_weights[None, :, None]).astype(jnp.bfloat16)
    ch, lats, m_win = fourier.shape
    pairs, length = legendre.shape[1:]
    width = 256
    steps = length // width
    wave = jnp.transpose(weighted, (2, 0, 1)).reshape(m_win * ch, lats)
    own = pairs // n_lat
    chips = n_lat // 2
    cfg = (n_lat, n_lev, ch, lats, pairs, length, width, steps, m_win)
    dma = pltpu.SemaphoreType.DMA
    block = pairs // HALVES
    spectra, energy = pl.pallas_call(
        functools.partial(kernel, cfg),
        grid=(steps, HALVES),
        out_shape=(
            jax.ShapeDtypeStruct((own, ch, length), jnp.float32),
            jax.ShapeDtypeStruct((1, 1), jnp.float32),
        ),
        in_specs=[
            pl.BlockSpec(memory_space=pltpu.SMEM),
            pl.BlockSpec((m_win * ch, lats), lambda t, h: (0, 0)),
            pl.BlockSpec((lats, block, width), lambda t, h: (0, h, t)),
        ],
        out_specs=(
            pl.BlockSpec((own, ch, length), lambda t, h: (0, 0, 0)),
            pl.BlockSpec((1, 1), lambda t, h: (0, 0)),
        ),
        scratch_shapes=[
            pltpu.VMEM((pairs // GROUP, 2 * GROUP * ch, lats * GROUP), jnp.bfloat16),
            pltpu.VMEM((2, pairs, ch, width), jnp.float32),
            pltpu.VMEM((steps, pairs // 2, ch, width), jnp.float32),
            pltpu.VMEM((steps, pairs // 2, ch, width), jnp.float32),
            pltpu.VMEM((steps, chips - 1, own, ch, width), jnp.bfloat16),
            pltpu.VMEM((steps, chips - 1, own, ch, width), jnp.bfloat16),
            pltpu.VMEM((ch, width), jnp.float32),
            pltpu.VMEM((n_lat, 8, 128), jnp.float32),
            pltpu.VMEM((n_lev, 8, 128), jnp.float32),
            dma((steps,)),
            dma((steps,)),
            dma((steps, chips - 1)),
            dma((steps, chips - 1)),
            dma((n_lat - 1,)),
            dma((n_lat,)),
            dma((n_lev - 1,)),
            dma((n_lev,)),
        ],
        compiler_params=pltpu.CompilerParams(
            collective_id=0,
            has_side_effects=True,
            vmem_limit_bytes=60 * 1024 * 1024,
            dimension_semantics=("arbitrary", "arbitrary"),
        ),
    )(owner_pair, wave, legendre)
    return spectra, energy.reshape(())


def solution(mesh):
    return jax.shard_map(
        functools.partial(shards, mesh.shape["lat"], mesh.shape["lev"]),
        mesh=mesh,
        in_specs=(P("lev", "lat", None), P("lat"), P("lat", None, None), P()),
        out_specs=(P("lat", "lev", None), P()),
        check_vma=False,
    )
```

profile of v0, /device:TPU:0, one launch (start us, length us, event | category | flops | bytes accessed | tf_op | source)
XLA Modules:
  0.0 54.7 jit_solution(1792838654287882621)
XLA Ops:
  0.6 1.7 %fusion = bf16[128,16,320]{0,2,1:T(8,128)(2,1)S(1)} fusion(bf16[16,320,128]{2,1,0:T(8,128)(2,1)} %param.4, f32[320]{0:T(512)} %param.5), kind=kLoop, calls=%fused_computation.1 | loop fusion | flops 1966080 | bytes 2622720 | tf_op jit(solution)/shard_map/transpose | solution.py:231
  2.4 1.9 %copy.6 = bf16[128,16,320]{2,1,0:T(8,128)(2,1)} copy(bf16[128,16,320]{0,2,1:T(8,128)(2,1)S(1)} %fusion) | data formatting | bytes 2621440 | tf_op jit(solution)/shard_map/transpose | solution.py:231
  4.3 46.7 %shard_map.59 = (f32[8,16,1280]{2,1,0:T(8,128)}, f32[1,1]{1,0:T(1,128)}) custom-call(s32[64]{0:T(128)} %owner_ref.1, bf16[2048,320]{1,0:T(8,128)(2,1)} %bitcast.4, bf16[320,64,1280]{2,1,0:T(8,128)(2,1)} %leg_ref.1), custom_call_target="tpu_custom_call" | custom-call | tf_op jit(solution)/shard_map/pallas_call | solution.py:237
  51.0 2.0 %copy.9 = f32[8,16,1280]{2,1,0:T(8,128)} copy(f32[8,16,1280]{2,1,0:T(8,128)} %get-tuple-element.8) | data formatting | bytes 1310720
where the time goes:
time: 55.1 us; the launch traced here: 54.7 us
  Pallas kernels  46.7 us (85%)
  local copies, waits for them, and re-layouts  3.9 us (7%)
  between operations  2.41 us (4%)
  other arithmetic  1.72 us (3%)
    pallas_call x1, Pallas kernels, shards(): pl.pallas_call(functools.partial(kernel, cfg), grid=(steps, HALVES), out_...  46.7 us
    unnamed x1, local copies, waits for them, and re-layouts  1.97 us
    transpose x1, local copies, waits for them, and re-layouts, shards(): wave = jnp.transpose(weighted, (2, 0, 1)).reshape(m_win * ch, lats)  1.93 us
    transpose x1, other arithmetic, shards(): wave = jnp.transpose(weighted, (2, 0, 1)).reshape(m_win * ch, lats)  1.72 us

commit v1 on v0

v1 whole, which is shorter than its diff:
```python
import functools

import jax
import jax.numpy as jnp
from jax import lax
from jax.experimental import pallas as pl
from jax.experimental.pallas import tpu as pltpu
from jax.sharding import PartitionSpec as P

SPACING = 10
GROUP = 8
LANES = 128
BLOCK = 16
SLOTS = 10
MESH = pl.DeviceIdType.MESH


def remote(src, dst, send, recv, device):
    return pltpu.make_async_remote_copy(
        src_ref=src, dst_ref=dst, send_sem=send, recv_sem=recv, device_id=device, device_id_type=MESH
    )


def kernel(
    cfg,
    owner_ref,
    weight_ref,
    wave_ref,
    leg_ref,
    out_ref,
    energy_ref,
    wave,
    turned,
    pieces,
    lhs,
    ring,
    both,
    part,
    pair_out,
    pair_in,
    chip_out,
    chip_in,
    esum,
    shares,
    wave_sem,
    ring_sem,
    pair_send,
    pair_recv,
    chip_send,
    chip_recv,
    share_send,
    share_recv,
):
    n_lat, n_lev, ch, lats, pairs, length, m_win, chunks = cfg
    lat = lax.axis_index("lat")
    lev = lax.axis_index("lev")
    core = lax.rem(lat, 2)
    chip = lat // 2
    chips = n_lat // 2
    own = pairs // n_lat
    rows = GROUP * ch
    groups = pairs // GROUP
    depth = lats * GROUP
    half = m_win // 2
    n_dev = n_lat * n_lev
    me = lat * n_lev + lev
    per_chunk = pairs // BLOCK
    blocks = [(c, h) for c in range(len(chunks)) for h in range(per_chunk)]
    barrier = pltpu.get_barrier_semaphore()

    def load(b):
        c, h = blocks[b]
        col, width = chunks[c]
        slot = b % SLOTS
        return pltpu.make_async_copy(
            leg_ref.at[:, h * BLOCK : (h + 1) * BLOCK, col : col + width],
            ring.at[slot, :, :, :width],
            ring_sem.at[slot],
        )

    wave_copy = pltpu.make_async_copy(wave_ref, wave, wave_sem)
    wave_copy.start()
    for b in range(min(SLOTS, len(blocks))):
        load(b).start()

    def device(i):
        return (i // n_lev, lax.rem(i, n_lev))

    def greet(d, carry):
        pl.semaphore_signal(
            barrier, inc=1, device_id=device(lax.rem(me + d, n_dev)), device_id_type=MESH
        )
        return carry

    lax.fori_loop(1, n_dev, greet, 0)
    esum[...] = jnp.zeros_like(esum)

    padded = turned.shape[1]
    weight = jnp.broadcast_to(weight_ref[...], (GROUP, lats))
    if padded > lats:
        weight = jnp.concatenate([weight, jnp.zeros((GROUP, padded - lats), jnp.float32)], 1)
    rest = weight
    for i in range(3):
        piece = rest.astype(jnp.bfloat16).astype(jnp.float32)
        pieces[i * GROUP : (i + 1) * GROUP, :] = piece
        rest = rest - piece

    wave_copy.wait()
    for c in range(ch):
        x = wave[c]
        if padded > lats:
            x = jnp.concatenate([x, jnp.zeros((padded - lats, m_win), x.dtype)], 0)
        x = x.T
        for side in range(2):
            turned[side * half * ch + c * half : side * half * ch + (c + 1) * half, :] = x[
                side * half : (side + 1) * half
            ]

    tile = 512 if depth % 512 == 0 else depth
    at_once = 4

    def build(side):
        for q in range(depth // tile):
            first = q * tile // GROUP
            base = first // LANES * LANES
            src = lax.broadcasted_iota(jnp.int32, (LANES, tile), 0)
            dst = lax.broadcasted_iota(jnp.int32, (LANES, tile), 1)
            spread = (src == dst // GROUP + (first - base)).astype(jnp.float32).astype(jnp.bfloat16)
            w = jnp.dot(
                pieces[:, base : base + LANES].astype(jnp.bfloat16), spread,
                preferred_element_type=jnp.float32,
            )
            w = w[:GROUP] + w[GROUP : 2 * GROUP] + w[2 * GROUP :]
            row = lax.broadcasted_iota(jnp.int32, (GROUP, tile), 0)
            col = lax.rem(lax.broadcasted_iota(jnp.int32, (GROUP, tile), 1), GROUP)
            w = jnp.where(row == (col if side == 0 else GROUP - 1 - col), w, 0.0)
            for c in range(0, ch, at_once):
                start = side * half * ch + c * half
                x = jnp.dot(
                    turned[start : start + at_once * half, base : base + LANES], spread,
                    preferred_element_type=jnp.float32,
                ).reshape(at_once, groups, GROUP, tile)
                for j in range(groups):
                    g = j if side == 0 else groups - 1 - j
                    lhs[
                        g,
                        side * rows + c * GROUP : side * rows + (c + at_once) * GROUP,
                        q * tile : (q + 1) * tile,
                    ] = (x[:, j] * w[None]).reshape(at_once * GROUP, tile).astype(jnp.bfloat16)

    build(0)
    build(1)

    def multiply(b):
        c, h = blocks[b]
        col, width = chunks[c]
        load(b).wait()
        for i in range(BLOCK // GROUP):
            g = h * (BLOCK // GROUP) + i
            limits = [length - SPACING * p - SPACING // 2 for p in range(g * GROUP, (g + 1) * GROUP)]
            low = col < max(limits)
            high = col + width > min(limits)
            x = lhs[g] if low and high else lhs[g, :rows] if low else lhs[g, rows:]
            rhs = ring[b % SLOTS, :, i * GROUP : (i + 1) * GROUP, :width].reshape(depth, width)
            y = jnp.dot(x, rhs, preferred_element_type=jnp.float32)
            for u in range(width // LANES):
                both[i, u, : y.shape[0]] = y[:, u * LANES : (u + 1) * LANES]
            for u in range(width // LANES):
                ids = col + u * LANES + lax.broadcasted_iota(jnp.int32, (ch, LANES), 1)
                for k in range(GROUP):
                    first = k if low else GROUP - 1 - k
                    z = both[i, u, pl.ds(first, ch, stride=GROUP), :]
                    if low and high:
                        z = jnp.where(
                            ids < limits[k], z,
                            both[i, u, pl.ds(rows + GROUP - 1 - k, ch, stride=GROUP), :],
                        )
                    part[c % 2, u, g * GROUP + k] = z
        if b + SLOTS < len(blocks):
            load(b + SLOTS).start()

    def units(c):
        first = sum(width for _, width in chunks[:c]) // LANES
        return first, chunks[c][1] // LANES

    def pair_copy(c):
        first, count = units(c)
        span = pl.ds(first, count)
        return remote(
            pair_out.at[span], pair_in.at[span], pair_send.at[c], pair_recv.at[c],
            (2 * chip + 1 - core, lev),
        )

    def chip_copy(c, d):
        first, count = units(c)
        span = pl.ds(first, count)
        return remote(
            chip_out.at[span, d - 1], chip_in.at[span, d - 1],
            chip_send.at[c, d - 1], chip_recv.at[c, d - 1],
            (2 * lax.rem(chip + d, chips) + core, lev),
        )

    def to_partner(c):
        first, count = units(c)
        for d in range(chips):
            q = lax.rem(chip + d, chips)
            for o in range(own):
                pair_id = owner_ref[(2 * q + 1 - core) * own + o]
                for u in range(count):
                    pair_out[first + u, d * own + o] = part[c % 2, u, pair_id]
        pair_copy(c).start()

    order = list(range(1, chips)) + [0]

    def to_chips(c):
        first, count = units(c)
        col, _ = chunks[c]
        pair_copy(c).wait_recv()
        for d in order:
            q = lax.rem(chip + d, chips)
            for o in range(own):
                pair_id = owner_ref[(2 * q + core) * own + o]
                for u in range(count):
                    total = part[c % 2, u, pair_id] + pair_in[first + u, d * own + o]
                    if d:
                        chip_out[first + u, d - 1, o] = total.astype(jnp.bfloat16)
                    else:
                        out_ref[o, :, col + u * LANES : col + (u + 1) * LANES] = total
            if d:
                chip_copy(c, d).start()

    channel = lev * ch + lax.broadcasted_iota(jnp.int32, (ch, LANES), 0)
    factor = 1.0 + 2.0 * (channel // 2).astype(jnp.float32) / (ch * n_lev // 2 - 1)

    def collect(c):
        first, count = units(c)
        col, _ = chunks[c]
        for d in range(1, chips):
            chip_copy(c, d).wait_recv()
        acc = jnp.zeros((ch, LANES), jnp.float32)
        for o in range(own):
            for u in range(count):
                cols = slice(col + u * LANES, col + (u + 1) * LANES)
                total = out_ref[o, :, cols]
                for d in range(1, chips):
                    total = total + chip_in[first + u, d - 1, o].astype(jnp.float32)
                out_ref[o, :, cols] = total
                acc = acc + total * total
        esum[...] += acc * factor

    collected = 0
    for b in range(len(blocks)):
        multiply(b)
        c, h = blocks[b]
        if h == per_chunk - 1:
            if c == 0:
                pl.semaphore_wait(barrier, n_dev - 1)
            to_partner(c)
            if c >= 3:
                collect(collected)
                collected += 1
        if h == 1 and c >= 1:
            to_chips(c - 1)
    while collected < len(chunks) - 1:
        collect(collected)
        collected += 1
    to_chips(len(chunks) - 1)
    collect(len(chunks) - 1)

    shares[me] = jnp.sum(esum[...], axis=0, keepdims=True)

    def share_copy(d):
        return remote(
            shares.at[me], shares.at[me], share_send, share_recv, device(lax.rem(me + d, n_dev))
        )

    def spread_share(d, carry):
        share_copy(d).start()
        return carry

    lax.fori_loop(1, n_dev, spread_share, 0)
    most = shares.at[pl.ds(0, n_dev - 1)]
    every = remote(most, most, share_send, share_recv, device(lax.rem(me + 1, n_dev)))
    every.wait_recv()
    energy_ref[...] = jnp.full((1, 1), jnp.sum(shares[...])) / (pairs * ch * n_lev * length)
    every.wait_send()
    for c in range(len(chunks)):
        pair_copy(c).wait_send()
        for d in range(1, chips):
            chip_copy(c, d).wait_send()


def shards(n_lat, n_lev, fourier, quad_weights, legendre, owner_pair):
    ch, lats, m_win = fourier.shape
    pairs, length = legendre.shape[1:]
    width = 256
    chunks = tuple((col, width) for col in range(0, length, width))
    own = pairs // n_lat
    chips = n_lat // 2
    n_dev = n_lat * n_lev
    count = length // LANES
    padded = -(-lats // LANES) * LANES
    depth = lats * GROUP
    cfg = (n_lat, n_lev, ch, lats, pairs, length, m_win, chunks)
    dma = pltpu.SemaphoreType.DMA
    vmem = pltpu.VMEM
    spectra, energy = pl.pallas_call(
        functools.partial(kernel, cfg),
        out_shape=(
            jax.ShapeDtypeStruct((own, ch, length), jnp.float32),
            jax.ShapeDtypeStruct((1, 1), jnp.float32),
        ),
        in_specs=[
            pl.BlockSpec(memory_space=pltpu.SMEM),
            pl.BlockSpec(memory_space=pltpu.VMEM),
            pl.BlockSpec(memory_space=pl.ANY),
            pl.BlockSpec(memory_space=pl.ANY),
        ],
        out_specs=(
            pl.BlockSpec(memory_space=pltpu.VMEM),
            pl.BlockSpec(memory_space=pltpu.VMEM),
        ),
        scratch_shapes=[
            vmem((ch, lats, m_win), jnp.bfloat16),
            vmem((ch * m_win, padded), jnp.bfloat16),
            vmem((3 * GROUP, padded), jnp.float32),
            vmem((pairs // GROUP, 2 * GROUP * ch, depth), jnp.bfloat16),
            vmem((SLOTS, lats, BLOCK, width), jnp.bfloat16),
            vmem((BLOCK // GROUP, width // LANES, 2 * GROUP * ch, LANES), jnp.float32),
            vmem((2, width // LANES, pairs, ch, LANES), jnp.float32),
            vmem((count, pairs // 2, ch, LANES), jnp.float32),
            vmem((count, pairs // 2, ch, LANES), jnp.float32),
            vmem((count, chips - 1, own, ch, LANES), jnp.bfloat16),
            vmem((count, chips - 1, own, ch, LANES), jnp.bfloat16),
            vmem((ch, LANES), jnp.float32),
            vmem((n_dev, 1, LANES), jnp.float32),
            dma,
            dma((SLOTS,)),
            dma((len(chunks),)),
            dma((len(chunks),)),
            dma((len(chunks), chips - 1)),
            dma((len(chunks), chips - 1)),
            dma,
            dma,
        ],
        compiler_params=pltpu.CompilerParams(
            collective_id=0,
            has_side_effects=True,
            vmem_limit_bytes=60 * 1024 * 1024,
        ),
    )(owner_pair, quad_weights.reshape(1, lats), fourier, legendre)
    return spectra, energy.reshape(())


def solution(mesh):
    return jax.shard_map(
        functools.partial(shards, mesh.shape["lat"], mesh.shape["lev"]),
        mesh=mesh,
        in_specs=(P("lev", "lat", None), P("lat"), P("lat", None, None), P()),
        out_specs=(P("lat", "lev", None), P()),
        check_vma=False,
    )
```

time: 55.1 us -> 44.7 us (0.81)
  Pallas kernels: 46.7 us -> 38.8 us
  other arithmetic: 1.72 us -> 0 us
  local copies, waits for them, and re-layouts: 3.9 us -> 3.22 us
    pallas_call x1, Pallas kernels: 46.7 us -> 38.8 us  [shards(): pl.pallas_call(functools.partial(kernel, cfg), out_shape=(jax.ShapeDtypeS...]
    transpose x1 -> x0, local copies, waits for them, and re-layouts: 1.93 us -> none  [shards(): wave = jnp.transpose(weighted, (2, 0, 1)).reshape(m_win * ch, lats)]
    transpose x1 -> x0, other arithmetic: 1.72 us -> none  [shards(): wave = jnp.transpose(weighted, (2, 0, 1)).reshape(m_win * ch, lats)]
    reshape x0 -> x1, local copies, waits for them, and re-layouts: none -> 1.25 us  [shards(): quad_weights.reshape(1, lats)]
where the time goes in v1:
time: 44.7 us; the launch traced here: 44.4 us
  Pallas kernels  38.8 us (87%)
  local copies, waits for them, and re-layouts  3.22 us (7%)
  between operations  2.39 us (5%)
    pallas_call x1, Pallas kernels, shards(): pl.pallas_call(functools.partial(kernel, cfg), out_shape=(jax.ShapeDtypeS...  38.8 us
    unnamed x1, local copies, waits for them, and re-layouts  1.97 us
    reshape x1, local copies, waits for them, and re-layouts, shards(): quad_weights.reshape(1, lats)  1.25 us

profile of v1, /device:TPU:0, one launch (start us, length us, event | category | flops | bytes accessed | tf_op | source)
XLA Modules:
  0.0 44.4 jit_solution(15441409514035640612)
XLA Ops:
  0.6 1.2 %reshape.10.weight_ref = f32[1,320]{1,0:T(1,128)} reshape(f32[320]{0:T(512)} %param.5) | data formatting | bytes 2560 | tf_op jit(solution)/shard_map/reshape | solution.py:351
  1.9 38.8 %shard_map.59 = (f32[8,16,1280]{2,1,0:T(8,128)}, f32[1,1]{1,0:T(1,128)}) custom-call(s32[64]{0:T(128)} %owner_ref.1, f32[1,320]{1,0:T(1,128)} %reshape.10.weight_ref, bf16[16,320,128]{2,1,0:T(8,128)(2,1)} %wave_ref.1, bf16[320,64,1280]{2,1,0:T(8,128)(2,1)} %leg_ref.1), custom_call_target="tpu_custom_call" | custom-call | tf_op jit(solution)/shard_map/pallas_call | solution.py:307
  40.7 2.0 %copy.8 = f32[8,16,1280]{2,1,0:T(8,128)} copy(f32[8,16,1280]{2,1,0:T(8,128)} %get-tuple-element.8) | data formatting | bytes 1310720

commit v2 on v1

--- a/solution.py
+++ b/solution.py
@@ -11,7 +11,10 @@
 GROUP = 8
 LANES = 128
 BLOCK = 16
-SLOTS = 10
+SLOTS = 9
+HELD = 3
+NEAR = 64
+LATE = 3
 MESH = pl.DeviceIdType.MESH
 
 
@@ -23,13 +26,15 @@
 
 def kernel(
     cfg,
-    owner_ref,
+    owner_hbm,
     weight_ref,
     wave_ref,
     leg_ref,
     out_ref,
     energy_ref,
+    owner_ref,
     wave,
+    row,
     turned,
     pieces,
     lhs,
@@ -43,6 +48,8 @@
     esum,
     shares,
     wave_sem,
+    row_sem,
+    owner_sem,
     ring_sem,
     pair_send,
     pair_recv,
@@ -80,23 +87,33 @@
 
     wave_copy = pltpu.make_async_copy(wave_ref, wave, wave_sem)
     wave_copy.start()
+    row_copy = pltpu.make_async_copy(weight_ref, row.at[0], row_sem)
+    row_copy.start()
+    owner_copy = pltpu.make_async_copy(owner_hbm, owner_ref, owner_sem)
+    owner_copy.start()
     for b in range(min(SLOTS, len(blocks))):
         load(b).start()
 
-    def device(i):
-        return (i // n_lev, lax.rem(i, n_lev))
-
-    def greet(d, carry):
-        pl.semaphore_signal(
-            barrier, inc=1, device_id=device(lax.rem(me + d, n_dev)), device_id_type=MESH
-        )
-        return carry
-
-    lax.fori_loop(1, n_dev, greet, 0)
+    def others(act):
+        if n_dev <= NEAR:
+            for i in range(1, n_dev):
+                act(lax.rem(lat + i // n_lev, n_lat), lax.rem(lev + i % n_lev, n_lev))
+        else:
+            def step(i, carry):
+                act(lax.rem(lat + i // n_lev, n_lat), lax.rem(lev + lax.rem(i, n_lev), n_lev))
+                return carry
+
+            lax.fori_loop(1, n_dev, step, 0)
+
+    others(
+        lambda i, j: pl.semaphore_signal(barrier, inc=1, device_id=(i, j), device_id_type=MESH)
+    )
     esum[...] = jnp.zeros_like(esum)
 
     padded = turned.shape[1]
-    weight = jnp.broadcast_to(weight_ref[...], (GROUP, lats))
+    row_copy.wait()
+    owner_copy.wait()
+    weight = jnp.broadcast_to(row[...], (GROUP, lats))
     if padded > lats:
         weight = jnp.concatenate([weight, jnp.zeros((GROUP, padded - lats), jnp.float32)], 1)
     rest = weight
@@ -131,9 +148,9 @@
                 preferred_element_type=jnp.float32,
             )
             w = w[:GROUP] + w[GROUP : 2 * GROUP] + w[2 * GROUP :]
-            row = lax.broadcasted_iota(jnp.int32, (GROUP, tile), 0)
+            line = lax.broadcasted_iota(jnp.int32, (GROUP, tile), 0)
             col = lax.rem(lax.broadcasted_iota(jnp.int32, (GROUP, tile), 1), GROUP)
-            w = jnp.where(row == (col if side == 0 else GROUP - 1 - col), w, 0.0)
+            w = jnp.where(line == (col if side == 0 else GROUP - 1 - col), w, 0.0)
             for c in range(0, ch, at_once):
                 start = side * half * ch + c * half
                 x = jnp.dot(
@@ -183,11 +200,12 @@
         first = sum(width for _, width in chunks[:c]) // LANES
         return first, chunks[c][1] // LANES
 
-    def pair_copy(c):
-        first, count = units(c)
-        span = pl.ds(first, count)
+    order = list(range(chips - 1, -1, -1))
+
+    def pair_copy(c, d):
+        span = (c % HELD, pl.ds(0, chunks[c][1] // LANES), pl.ds(d * own, own))
         return remote(
-            pair_out.at[span], pair_in.at[span], pair_send.at[c], pair_recv.at[c],
+            pair_out.at[span], pair_in.at[span], pair_send.at[c, d], pair_recv.at[c, d],
             (2 * chip + 1 - core, lev),
         )
 
@@ -201,27 +219,27 @@
         )
 
     def to_partner(c):
-        first, count = units(c)
-        for d in range(chips):
+        _, count = units(c)
+        for d in order:
+            if c >= HELD:
+                pair_copy(c - HELD, d).wait_send()
             q = lax.rem(chip + d, chips)
             for o in range(own):
                 pair_id = owner_ref[(2 * q + 1 - core) * own + o]
                 for u in range(count):
-                    pair_out[first + u, d * own + o] = part[c % 2, u, pair_id]
-        pair_copy(c).start()
-
-    order = list(range(1, chips)) + [0]
+                    pair_out[c % HELD, u, d * own + o] = part[c % 2, u, pair_id]
+            pair_copy(c, d).start()
 
     def to_chips(c):
         first, count = units(c)
         col, _ = chunks[c]
-        pair_copy(c).wait_recv()
         for d in order:
+            pair_copy(c, d).wait_recv()
             q = lax.rem(chip + d, chips)
             for o in range(own):
                 pair_id = owner_ref[(2 * q + core) * own + o]
                 for u in range(count):
-                    total = part[c % 2, u, pair_id] + pair_in[first + u, d * own + o]
+                    total = part[c % 2, u, pair_id] + pair_in[c % HELD, u, d * own + o]
                     if d:
                         chip_out[first + u, d - 1, o] = total.astype(jnp.bfloat16)
                     else:
@@ -248,52 +266,47 @@
                 acc = acc + total * total
         esum[...] += acc * factor
 
-    collected = 0
+    last = len(chunks) - 1
     for b in range(len(blocks)):
         multiply(b)
         c, h = blocks[b]
+        if h == per_chunk // 2 and c >= 1:
+            to_chips(c - 1)
         if h == per_chunk - 1:
             if c == 0:
                 pl.semaphore_wait(barrier, n_dev - 1)
             to_partner(c)
-            if c >= 3:
-                collect(collected)
-                collected += 1
-        if h == 1 and c >= 1:
-            to_chips(c - 1)
-    while collected < len(chunks) - 1:
-        collect(collected)
-        collected += 1
-    to_chips(len(chunks) - 1)
-    collect(len(chunks) - 1)
+            if c >= LATE:
+                collect(c - LATE)
+    for c in range(max(last + 1 - LATE, 0), max(last - 2, 0)):
+        collect(c)
+    to_chips(last)
+    for c in range(max(last - 2, 0), last + 1):
+        collect(c)
 
     shares[me] = jnp.sum(esum[...], axis=0, keepdims=True)
-
-    def share_copy(d):
-        return remote(
-            shares.at[me], shares.at[me], share_send, share_recv, device(lax.rem(me + d, n_dev))
-        )
-
-    def spread_share(d, carry):
-        share_copy(d).start()
-        return carry
-
-    lax.fori_loop(1, n_dev, spread_share, 0)
+    others(
+        lambda i, j: remote(
+            shares.at[me], shares.at[me], share_send, share_recv, (i, j)
+        ).start()
+    )
     most = shares.at[pl.ds(0, n_dev - 1)]
-    every = remote(most, most, share_send, share_recv, device(lax.rem(me + 1, n_dev)))
+    every = remote(most, most, share_send, share_recv, (2 * chip + 1 - core, lev))
     every.wait_recv()
     energy_ref[...] = jnp.full((1, 1), jnp.sum(shares[...])) / (pairs * ch * n_lev * length)
     every.wait_send()
     for c in range(len(chunks)):
-        pair_copy(c).wait_send()
-        for d in range(1, chips):
-            chip_copy(c, d).wait_send()
+        for d in range(chips):
+            if c > last - HELD:
+                pair_copy(c, d).wait_send()
+            if d:
+                chip_copy(c, d).wait_send()
 
 
 def shards(n_lat, n_lev, fourier, quad_weights, legendre, owner_pair):
     ch, lats, m_win = fourier.shape
     pairs, length = legendre.shape[1:]
-    width = 256
+    width = 2 * LANES
     chunks = tuple((col, width) for col in range(0, length, width))
     own = pairs // n_lat
     chips = n_lat // 2
@@ -311,33 +324,37 @@
             jax.ShapeDtypeStruct((1, 1), jnp.float32),
         ),
         in_specs=[
-            pl.BlockSpec(memory_space=pltpu.SMEM),
-            pl.BlockSpec(memory_space=pltpu.VMEM),
-            pl.BlockSpec(memory_space=pl.ANY),
-            pl.BlockSpec(memory_space=pl.ANY),
+            pl.BlockSpec(memory_space=pltpu.HBM),
+            pl.BlockSpec(memory_space=pltpu.HBM),
+            pl.BlockSpec(memory_space=pltpu.HBM),
+            pl.BlockSpec(memory_space=pltpu.HBM),
         ],
         out_specs=(
             pl.BlockSpec(memory_space=pltpu.VMEM),
             pl.BlockSpec(memory_space=pltpu.VMEM),
         ),
         scratch_shapes=[
+            pltpu.SMEM((pairs,), jnp.int32),
             vmem((ch, lats, m_win), jnp.bfloat16),
+            vmem((1, lats), jnp.float32),
             vmem((ch * m_win, padded), jnp.bfloat16),
             vmem((3 * GROUP, padded), jnp.float32),
             vmem((pairs // GROUP, 2 * GROUP * ch, depth), jnp.bfloat16),
             vmem((SLOTS, lats, BLOCK, width), jnp.bfloat16),
             vmem((BLOCK // GROUP, width // LANES, 2 * GROUP * ch, LANES), jnp.float32),
             vmem((2, width // LANES, pairs, ch, LANES), jnp.float32),
-            vmem((count, pairs // 2, ch, LANES), jnp.float32),
-            vmem((count, pairs // 2, ch, LANES), jnp.float32),
+            vmem((HELD, width // LANES, pairs // 2, ch, LANES), jnp.float32),
+            vmem((HELD, width // LANES, pairs // 2, ch, LANES), jnp.float32),
             vmem((count, chips - 1, own, ch, LANES), jnp.bfloat16),
             vmem((count, chips - 1, own, ch, LANES), jnp.bfloat16),
             vmem((ch, LANES), jnp.float32),
             vmem((n_dev, 1, LANES), jnp.float32),
             dma,
+            dma,
+            dma,
             dma((SLOTS,)),
-            dma((len(chunks),)),
-            dma((len(chunks),)),
+            dma((len(chunks), chips)),
+            dma((len(chunks), chips)),
             dma((len(chunks), chips - 1)),
             dma((len(chunks), chips - 1)),
             dma,
@@ -346,9 +363,9 @@
         compiler_params=pltpu.CompilerParams(
             collective_id=0,
             has_side_effects=True,
-            vmem_limit_bytes=60 * 1024 * 1024,
+            vmem_limit_bytes=53 * 1024 * 1024,
         ),
-    )(owner_pair, quad_weights.reshape(1, lats), fourier, legendre)
+    )(owner_pair, quad_weights, fourier, legendre)
     return spectra, energy.reshape(())
 
 

time: 44.7 us -> 39.8 us (0.89)
  Pallas kernels: 38.8 us -> 35 us
  local copies, waits for them, and re-layouts: 3.22 us -> 2.17 us
    pallas_call x1, Pallas kernels: 38.8 us -> 35 us  [shards(): pl.pallas_call(functools.partial(kernel, cfg), out_shape=(jax.ShapeDtypeS...]
    reshape x1 -> x0, local copies, waits for them, and re-layouts: 1.25 us -> none  [shards(): quad_weights.reshape(1, lats)]
    unnamed x1 -> x5, local copies, waits for them, and re-layouts: 1.97 us -> 2.17 us
where the time goes in v2:
time: 39.8 us; the launch traced here: 39.6 us
  Pallas kernels  35 us (88%)
  between operations  2.41 us (6%)
  local copies, waits for them, and re-layouts  2.17 us (5%)
    pallas_call x1, Pallas kernels, shards(): pl.pallas_call(functools.partial(kernel, cfg), out_shape=(jax.ShapeDtypeS...  35 us
    unnamed x5, local copies, waits for them, and re-layouts  2.17 us

profile of v2, /device:TPU:0, one launch (start us, length us, event | category | flops | bytes accessed | tf_op | source)
XLA Modules:
  0.0 39.6 jit_solution(6349052596629219860)
XLA Ops:
  0.6 0.0 copy-start
  0.6 0.7 %copy-done = f32[320]{0:T(512)S(1)} copy-done((f32[320]{0:T(512)S(1)}, f32[320]{0:T(512)}, u32[]{:S(2)}) %copy-start) | copy-done | bytes 1304
  1.3 0.0 copy-start.1
  1.3 0.7 %copy-done.1 = s32[64]{0:T(128)S(1)} copy-done((s32[64]{0:T(128)S(1)}, s32[64]{0:T(128)}, u32[]{:S(2)}) %copy-start.1) | copy-done | bytes 280
  2.0 35.0 %shard_map.59 = (f32[8,16,1280]{2,1,0:T(8,128)S(1)}, f32[1,1]{1,0:T(1,128)}) custom-call(s32[64]{0:T(128)S(1)} %copy-done.1, f32[320]{0:T(512)S(1)} %copy-done, bf16[16,320,128]{2,1,0:T(8,128)(2,1)} %wave_ref.1, bf16[320,64,1280]{2,1,0:T(8,128)(2,1)} %leg_ref.1), custom_call_target="tpu_custom_call" | custom-call | tf_op jit(solution)/shard_map/pallas_call | solution.py:320
  37.0 0.8 %copy.8 = f32[8,16,1280]{2,1,0:T(8,128)} copy(f32[8,16,1280]{2,1,0:T(8,128)S(1)} %get-tuple-element.8) | data formatting | bytes 1310720
Async XLA Ops:
  0.6 0.7 %copy-start = (f32[320]{0:T(512)S(1)}, f32[320]{0:T(512)}, u32[]{:S(2)}) copy-start(f32[320]{0:T(512)} %weight_ref.1) | copy-start | bytes 3844
  1.3 0.7 %copy-start.1 = (s32[64]{0:T(128)S(1)}, s32[64]{0:T(128)}, u32[]{:S(2)}) copy-start(s32[64]{0:T(128)} %owner_hbm.1) | copy-start | bytes 772

commit v3 on v2

--- a/solution.py
+++ b/solution.py
@@ -317,6 +317,10 @@
     cfg = (n_lat, n_lev, ch, lats, pairs, length, m_win, chunks)
     dma = pltpu.SemaphoreType.DMA
     vmem = pltpu.VMEM
+    taken = [
+        pltpu.with_memory_space_constraint(x, pltpu.HBM)
+        for x in (owner_pair, quad_weights, fourier, legendre)
+    ]
     spectra, energy = pl.pallas_call(
         functools.partial(kernel, cfg),
         out_shape=(
@@ -365,7 +369,7 @@
             has_side_effects=True,
             vmem_limit_bytes=53 * 1024 * 1024,
         ),
-    )(owner_pair, quad_weights, fourier, legendre)
+    )(*taken)
     return spectra, energy.reshape(())
 
 

time: 39.8 us -> 38.3 us (0.962)
  local copies, waits for them, and re-layouts: 2.17 us -> 0.84 us
    unnamed x5 -> x1, local copies, waits for them, and re-layouts: 2.17 us -> 0.84 us
where the time goes in v3:
time: 38.3 us; the launch traced here: 38.1 us
  Pallas kernels  35 us (91%)
  between operations  2.33 us (6%)
  local copies, waits for them, and re-layouts  0.84 us (2%)
    pallas_call x1, Pallas kernels, shards(): pl.pallas_call(functools.partial(kernel, cfg), out_shape=(jax.ShapeDtypeS...  35 us
    unnamed x1, local copies, waits for them, and re-layouts  0.84 us

profile of v3, /device:TPU:0, one launch (start us, length us, event | category | flops | bytes accessed | tf_op | source)
XLA Modules:
  0.0 38.1 jit_solution(802231335288766238)
XLA Ops:
  0.6 35.0 %shard_map.59 = (f32[8,16,1280]{2,1,0:T(8,128)S(1)}, f32[1,1]{1,0:T(1,128)}) custom-call(s32[64]{0:T(128)} %owner_hbm.1, f32[320]{0:T(512)} %weight_ref.1, bf16[16,320,128]{2,1,0:T(8,128)(2,1)} %wave_ref.1, bf16[320,64,1280]{2,1,0:T(8,128)(2,1)} %leg_ref.1), custom_call_target="tpu_custom_call" | custom-call | tf_op jit(solution)/shard_map/pallas_call | solution.py:324
  35.6 0.8 %copy.8 = f32[8,16,1280]{2,1,0:T(8,128)} copy(f32[8,16,1280]{2,1,0:T(8,128)S(1)} %get-tuple-element.8) | data formatting | bytes 1310720
